TPU v7x, 32 devices: a whole 2x2x4 slice. The times are simulated.
32 devices in a mesh: pq: 8 (over z, x), hh: 4 (over y, core).
Axes of the slice: x: 2, y: 2, z: 4, core: 2. Of those that a mesh axis runs over, the one named last changes fastest.
Arguments:
- amplitudes: bfloat16 [4096, 2048], P('hh', 'pq'), may hold values from -6 to 6
- integrals: bfloat16 [4096, 2048], P('hh', 'pq'), may hold values from -0.001953125 to 0.001953125
- left_amps: bfloat16 [8, 4096, 1024], P(None, 'hh', 'pq'), may hold values from -6 to 6
Outputs:
- sigma_ladder: bfloat16 [8, 4096, 1024], P(None, 'hh', 'pq')
- subspace: float32 [8, 8], replicated
All inputs are finite; a program needn't handle non-finite values.
Results may differ from a plain program's by a relative error of at most 0.0049.
Values may be sent and summed in bfloat16 or wider, within the bound.
A program may use at most 64 MiB of HBM per device.

v0:
```python
import math

import jax
import jax.numpy as jnp
from jax import lax
from jax.sharding import PartitionSpec as P

OCC_PAIRS = 4096


def body(amplitudes, integrals, left_amps):
    root_count = left_amps.shape[0]
    ab_cols = left_amps.shape[2]
    partial_t = lax.dot_general(
        integrals,
        lax.all_gather(amplitudes, "hh", axis=0, tiled=True),
        (((1,), (1,)), ((), ())),
        preferred_element_type=jnp.float32,
    )
    ladder_t = lax.psum_scatter(partial_t, "pq", scatter_dimension=1, tiled=True).astype(
        jnp.bfloat16
    )
    ladder_t = lax.all_gather(ladder_t, "pq", axis=1, tiled=True)
    rows_out = lax.dot_general(
        ladder_t,
        lax.all_gather(left_amps, "hh", axis=1, tiled=True),
        (((1,), (1,)), ((), ())),
        preferred_element_type=jnp.float32,
    )
    sigma_out = jnp.transpose(rows_out, (1, 0, 2)).astype(jnp.bfloat16)
    local_gram = jnp.dot(
        left_amps.reshape(root_count, -1),
        sigma_out.reshape(root_count, -1).T,
        preferred_element_type=jnp.float32,
    )
    factor = 1.0 / math.sqrt(OCC_PAIRS * ab_cols * lax.axis_size("pq"))
    subspace = lax.psum(local_gram, ("pq", "hh")) * factor
    return (sigma_out, subspace)


def solution(mesh):
    return jax.shard_map(
        body,
        mesh=mesh,
        in_specs=(P("hh", "pq"), P("hh", "pq"), P(None, "hh", "pq")),
        out_specs=(P(None, "hh", "pq"), P()),
        check_vma=False,
    )
```

profile of v0, /device:TPU:0, one launch (start us, length us, event | category | flops | bytes accessed | tf_op | source)
XLA Modules:
  0.0 574.4 jit_solution(7617182189609885000)
XLA Ops:
  7.2 0.0 copy-start
  7.2 0.0 all-gather.4.cloned.1.call-start
  7.2 0.7 all-gather.4.cloned.1.call-update
  7.9 0.0 reduce-scatter.2.cloned.1.call-start
  8.0 26.9 %all-gather.4.cloned.1.call-done = bf16[4096,256]{1,0:T(8,128)(2,1)} async-done(((bf16[1024,256]{1,0:T(8,128)(2,1)}), bf16[4096,256]{1,0:T(8,128)(2,1)}) %all-gather.4.cloned.1.call-update) | async-done | bytes 2097168 | tf_op jit(solution)/shard_map/all_gather | solution.py:16
  34.9 0.0 copy-done
  34.9 9.7 %fusion.12 = f32[1024,4096]{1,0:T(8,128)} fusion(bf16[1024,256]{1,0:T(8,128)(2,1)S(1)} %copy-done, bf16[4096,256]{1,0:T(8,128)(2,1)} %all-gather.4.cloned.1.call-done), kind=kOutput, calls=%fused_computation.8 | convolution fusion | flops 2147483648 | bytes 19398656 | tf_op jit(solution)/shard_map/dot_general | solution.py:14
  44.6 0.0 reduce-scatter.2.cloned.1.call-update
  44.6 0.0 all-gather.8.cloned.1.call-start
  44.6 0.7 all-gather.8.cloned.1.call-update
  45.3 0.0 all-gather.6.cloned.1.call-start
  45.4 279.5 %reduce-scatter.2.cloned.1.call-done = f32[1024,512]{1,0:T(8,128)} async-done(((f32[1024,4096]{1,0:T(8,128)}), f32[1024,512]{1,0:T(8,128)}) %reduce-scatter.2.cloned.1.call-update) | async-done | bytes 2097168 | tf_op jit(solution)/shard_map/reduce_scatter | solution.py:20
  324.9 2.7 convert_element_type.9
  327.6 0.0 all-gather.6.cloned.1.call-update
  327.7 0.0 copy-start.1
  327.7 56.3 %all-gather.8.cloned.1.call-done = bf16[8,4096,128]{2,1,0:T(8,128)(2,1)} async-done(((bf16[8,1024,128]{2,1,0:T(8,128)(2,1)}), bf16[8,4096,128]{2,1,0:T(8,128)(2,1)}) %all-gather.8.cloned.1.call-update) | async-done | bytes 8388624 | tf_op jit(solution)/shard_map/all_gather | solution.py:26
  383.9 127.4 %all-gather.6.cloned.1.call-done = bf16[1024,4096]{1,0:T(8,128)(2,1)} async-done(((bf16[1024,512]{1,0:T(8,128)(2,1)}), bf16[1024,4096]{1,0:T(8,128)(2,1)}) %all-gather.6.cloned.1.call-update) | async-done | bytes 8388624 | tf_op jit(solution)/shard_map/all_gather | solution.py:23
  511.4 13.7 %convert_bitcast_fusion = bf16[8,1024,128]{2,1,0:T(8,128)(2,1)S(1)} fusion(bf16[8,4096,128]{2,1,0:T(8,128)(2,1)} %all-gather.8.cloned.1.call-done, bf16[1024,4096]{1,0:T(8,128)(2,1)} %all-gather.6.cloned.1.call-done), kind=kOutput, calls=%fused_computation.5 | convolution fusion | flops 8590983168 | bytes 18874368 | tf_op jit(solution)/shard_map/dot_general | solution.py:24
  525.0 0.0 copy-start.2
  525.0 1.3 copy-done.2
  526.4 0.0 copy-done.1
  526.4 2.5 fusion.7
  528.9 38.4 %psum.7 = f32[8,8]{0,1:T(8,128)S(1)} all-reduce(f32[8,8]{0,1:T(8,128)S(1)} %fusion.7), channel_id=1, replica_groups=mesh['pq'=8,'hh'=4] {'pq','hh'}, use_global_device_ids=true, to_apply=%region_1.0 | all-reduce | flops 64 | bytes 512 | tf_op jit(solution)/shard_map/psum | solution.py:37
  567.2 0.7 copy.7
  (1 shorter events, 0.0 us)
Async XLA Ops:
  7.2 27.7 %copy-start = (bf16[1024,256]{1,0:T(8,128)(2,1)S(1)}, bf16[1024,256]{1,0:T(8,128)(2,1)}, u32[]{:S(2)}) copy-start(bf16[1024,256]{1,0:T(8,128)(2,1)} %param.4) | copy-start | bytes 1572868
  7.2 27.7 %all-gather.4.cloned.1.call-start = ((), (), s32[]{:S(2)}) async-start(), calls=%async_computation.1 | async-start | bytes 2621440 | tf_op jit(solution)/shard_map/all_gather | solution.py:16
  7.9 317.0 %reduce-scatter.2.cloned.1.call-start = ((), (), s32[]{:S(2)}) async-start(), calls=%async_computation.2 | async-start | bytes 18874368 | tf_op jit(solution)/shard_map/reduce_scatter | solution.py:20
  44.6 339.3 %all-gather.8.cloned.1.call-start = ((), (), s32[]{:S(2)}) async-start(), calls=%async_computation.4 | async-start | bytes 10485760 | tf_op jit(solution)/shard_map/all_gather | solution.py:26
  45.3 466.0 %all-gather.6.cloned.1.call-start = ((), (), s32[]{:S(2)}) async-start(), calls=%async_computation.3 | async-start | bytes 9437184 | tf_op jit(solution)/shard_map/all_gather | solution.py:23
  327.7 198.7 %copy-start.1 = (bf16[8,1024,128]{2,1,0:T(8,128)(2,1)S(1)}, bf16[8,1024,128]{2,1,0:T(8,128)(2,1)}, u32[]{:S(2)}) copy-start(bf16[8,1024,128]{2,1,0:T(8,128)(2,1)} %param.5) | copy-start | bytes 6291460
  525.0 1.3 copy-start.2
Sparse Core Ops, SparseCore 0:
  9.5 25.2 all-gather.3
  44.7 280.1 reduce-scatter.1
  326.5 57.3 all-gather.7
  386.4 124.9 all-gather.5
where the time goes:
time: 575 us; the launch traced here: 574 us
  waiting for transfers between devices  492 us (86%)
  blocking collectives  38.4 us (7%)
  matrix products  25.9 us (5%)
  between operations  13.8 us (2%)
    reduce_scatter x1, waiting for transfers between devices, body(): lax.psum_scatter(partial_t, 'pq', scatter_dimension=1, tiled=True)  280 us
    all_gather x1, waiting for transfers between devices, body(): ladder_t = lax.all_gather(ladder_t, 'pq', axis=1, tiled=True)  127 us
    all_gather x1, waiting for transfers between devices, body(): lax.all_gather(left_amps, 'hh', axis=1, tiled=True)  56.3 us
    psum x1, blocking collectives, body(): subspace = lax.psum(local_gram, ('pq', 'hh')) * factor  38.4 us
    all_gather x1, waiting for transfers between devices, body(): lax.all_gather(amplitudes, 'hh', axis=0, tiled=True)  26.9 us
    dot_general x1, matrix products, body(): lax.dot_general(ladder_t, lax.all_gather(left_amps, 'hh', axis=1, tiled=T...  13.7 us
  transfers between devices with their start and end apart: 4, of which 4 were waited for; matrix products, arithmetic and copies ran while one was open for 0% of the time, Pallas kernels for 0%

commit v1 on v0

v1 whole, which is shorter than its diff:
```python
import functools
import math

import jax
import jax.numpy as jnp
from jax import lax
from jax.experimental import pallas as pl
from jax.experimental.pallas import tpu as pltpu
from jax.sharding import PartitionSpec as P

MESH = pl.DeviceIdType.MESH
SLOTS = 4
TILE = 256


def remote(src, dst, send_sem, recv_sem, where):
    return pltpu.make_async_remote_copy(
        src_ref=src,
        dst_ref=dst,
        send_sem=send_sem,
        recv_sem=recv_sem,
        device_id=where,
        device_id_type=MESH,
    )


def kernel(
    npq, nhh, factor,
    t_ref, i_ref, l_ref, out_ref, sub_ref,
    tbuf, ibuf, lbuf, pbuf, sibr, ysend, yrecv, mbuf, acc, sig, gram, red,
    load_sem, out_sem, fwd_sem, blk_sem, sib_ssem, sib_rsem,
    y_ssem, y_rsem, m_ssem, m_rsem, r_ssem, r_rsem,
):
    nx = nhh // 2
    nz, ny = npq // nx, nhh // 2
    roots, rows, ab = l_ref.shape
    depth = t_ref.shape[1]
    half = depth // 2
    me, hh = lax.axis_index("pq"), lax.axis_index("hh")
    z, x = me // nx, me % nx
    y, c = hh // 2, hh % 2
    sibling = {"hh": y * 2 + (1 - c)}
    mine = pl.ds(pl.multiple_of(c * half, half), half)
    other = pl.ds(pl.multiple_of((1 - c) * half, half), half)

    loads = [
        pltpu.make_async_copy(t_ref, tbuf.at[me], load_sem.at[0]),
        pltpu.make_async_copy(i_ref, ibuf.at[me], load_sem.at[1]),
    ] + [
        pltpu.make_async_copy(
            l_ref.at[r], lbuf.at[:, pl.ds(r * ab, ab)], load_sem.at[2 + r]
        )
        for r in range(roots)
    ]
    for load in loads:
        load.start()

    barrier = pltpu.get_barrier_semaphore()
    for d in range(1, npq):
        pl.semaphore_signal(
            barrier, inc=1, device_id={"pq": (me + d) % npq}, device_id_type=MESH
        )
    for d in range(1, nhh):
        pl.semaphore_signal(
            barrier, inc=1, device_id={"hh": (hh + d) % nhh}, device_id_type=MESH
        )
    pl.semaphore_wait(barrier, npq + nhh - 2)

    below, above = z, nz - 1 - z
    paired = jnp.minimum(below, above)

    def column(i):
        step = (i + 1) // 2 if i % 2 else -(i // 2)
        side = jnp.where(above > below, 1, -1)
        return z + jnp.where(i <= 2 * paired, step, side * (i - paired))

    def block_copy(kind, blk, way):
        buf = (tbuf, ibuf)[kind].at[blk]
        to = me + (nx, -nx, 1, -1)[way]
        return remote(
            buf, buf, fwd_sem.at[kind, blk, way], blk_sem.at[kind, blk], {"pq": to}
        )

    def ways(zz, xx):
        if xx is None:
            return [
                (2, x < nx - 1),
                (3, x > 0),
                (0, (zz <= z) & (z < nz - 1)),
                (1, (zz >= z) & (z > 0)),
            ]
        if nx == 2:
            return []
        return [(2, (xx < x) & (x < nx - 1)), (3, (xx > x) & (x > 0))]

    def place(zz, xx):
        return zz * nx + (x if xx is None else xx)

    def forward(kind, zz, xx):
        blk = place(zz, xx)
        for way, cond in ways(zz, xx):
            @pl.when(cond)
            def _():
                block_copy(kind, blk, way).start()

    def sent(kind, zz, xx):
        blk = place(zz, xx)
        for way, cond in ways(zz, xx):
            @pl.when(cond)
            def _():
                block_copy(kind, blk, way).wait_send()

    def arrived(kind, zz, xx):
        block_copy(kind, place(zz, xx), 0).wait_recv()

    zs = [column(i) for i in range(nz)]
    xs = [(x + j) % nx for j in range(1, nx)]

    loads[0].wait()
    forward(0, zs[0], None)
    loads[1].wait()
    forward(1, zs[0], None)
    for load in loads[2:]:
        load.wait()

    order = []

    def sib_copy(k):
        s = k % SLOTS
        return remote(
            pbuf.at[s, other], sibr.at[s], sib_ssem.at[s], sib_rsem.at[s], sibling
        )

    def y_copy(k, d):
        s = k % SLOTS
        return remote(
            ysend.at[s], yrecv.at[s, d - 1], y_ssem.at[s, d - 1], y_rsem.at[s, d - 1],
            {"hh": (y + d) % ny * 2 + c},
        )

    def m_copy(k):
        buf = mbuf.at[:, place(*order[k]), mine]
        return remote(buf, buf, m_ssem.at[k], m_rsem.at[k], sibling)

    def stage1(k):
        if k >= SLOTS:
            m_copy(k - SLOTS).wait_recv()
        s = k % SLOTS
        pbuf[s] = lax.dot_general(
            tbuf[place(*order[k])], lbuf[...], (((0,), (0,)), ((), ())),
            preferred_element_type=jnp.float32,
        )
        sib_copy(k).start()

    def stage2(k):
        s = k % SLOTS
        sib_copy(k).wait_recv()
        total = pbuf[s, mine] + sibr[s]
        pbuf[s, mine] = total
        if k >= SLOTS:
            for d in range(1, ny):
                y_copy(k - SLOTS, d).wait_send()
        ysend[s] = total.astype(jnp.bfloat16)
        for d in range(1, ny):
            y_copy(k, d).start()

    def stage3(k):
        s = k % SLOTS
        total = pbuf[s, mine]
        for d in range(1, ny):
            y_copy(k, d).wait_recv()
            total = total + yrecv[s, d - 1].astype(jnp.float32)
        high = total.astype(jnp.bfloat16)
        mbuf[0, place(*order[k]), mine] = high
        mbuf[1, place(*order[k]), mine] = (total - high.astype(jnp.float32)).astype(
            jnp.bfloat16
        )
        m_copy(k).start()
        sib_copy(k).wait_send()

    def t_event(zz, xx):
        k = len(order)
        order.append((zz, xx))
        if k > 0:
            arrived(0, zz, xx)
            forward(0, zz, xx)
        stage1(k)
        if k >= 1:
            stage2(k - 1)
        if k >= 2:
            stage3(k - 2)

    for i in range(nz + 1):
        if i < nz:
            t_event(zs[i], None)
        if i >= 1:
            for xx in xs:
                t_event(zs[i - 1], xx)
        if i >= 2:
            arrived(1, zs[i - 1], None)
            forward(1, zs[i - 1], None)
    count = len(order)
    stage2(count - 1)
    stage3(count - 2)
    stage3(count - 1)

    for k in range(count):
        zz, xx = order[k]
        if k > count - 1 - SLOTS:
            m_copy(k).wait_recv()
        if xx is not None:
            arrived(1, zz, xx)
            forward(1, zz, xx)
        blk = place(zz, xx)

        @pl.loop(0, rows // TILE)
        def _(j):
            at = pl.ds(pl.multiple_of(j * TILE, TILE), TILE)
            prod = jnp.dot(
                ibuf[blk, at], mbuf[0, blk], preferred_element_type=jnp.float32
            ) + jnp.dot(ibuf[blk, at], mbuf[1, blk], preferred_element_type=jnp.float32)
            if k > 0:
                prod = acc[at] + prod
            if k < count - 1:
                acc[at] = prod
            else:
                sig[at] = prod.astype(jnp.bfloat16)

    outs = [
        pltpu.make_async_copy(
            sig.at[:, pl.ds(r * ab, ab)], out_ref.at[r], out_sem.at[r]
        )
        for r in range(roots)
    ]
    for copy in outs:
        copy.start()

    lanes = lax.broadcasted_iota(jnp.int32, (ab, roots * ab), 1) % ab
    diag = lanes == lax.broadcasted_iota(jnp.int32, (ab, roots * ab), 0)

    @pl.loop(0, roots)
    def _(r):
        cols = pl.ds(pl.multiple_of(r * ab, ab), ab)
        g = lax.dot_general(
            lbuf[:, cols], sig[...], (((0,), (0,)), ((), ())),
            preferred_element_type=jnp.float32,
        )
        gram[pl.ds(r, 1)] = jnp.sum(jnp.where(diag, g, 0.0), axis=0, keepdims=True)

    lane = lax.broadcasted_iota(jnp.int32, (roots, 128), 1)
    local = jnp.zeros((roots, 128), jnp.float32)
    for s in range(roots):
        one = jnp.sum(gram[:, s * ab : (s + 1) * ab], axis=1, keepdims=True)
        local = jnp.where(lane == s, one, local)

    base = 0
    for axis, at, n in (("hh", hh, nhh), ("pq", me, npq)):
        red[base] = local
        copies = [
            remote(
                red.at[base], red.at[base + d], r_ssem.at[base + d],
                r_rsem.at[base + d], {axis: (at + d) % n},
            )
            for d in range(1, n)
        ]
        for copy in copies:
            copy.start()
        for copy in copies:
            copy.wait_recv()
        for d in range(1, n):
            local = local + red[base + d]
        for copy in copies:
            copy.wait_send()
        base += n
    sub_ref[...] = local[:, :roots] * factor

    for k in range(count):
        sent(0, *order[k])
        sent(1, *order[k])
        m_copy(k).wait_send()
    for k in range(max(0, count - SLOTS), count):
        for d in range(1, ny):
            y_copy(k, d).wait_send()
    for copy in outs:
        copy.wait()


def solution(mesh):
    npq, nhh = mesh.shape["pq"], mesh.shape["hh"]

    def body(amplitudes, integrals, left_amps):
        roots, rows, ab = left_amps.shape
        depth = amplitudes.shape[1]
        half, wide = depth // 2, roots * ab
        ny = nhh // 2
        factor = 1.0 / math.sqrt(rows * nhh * ab * npq)
        bf16, f32, dma = jnp.bfloat16, jnp.float32, pltpu.SemaphoreType.DMA
        return pl.pallas_call(
            functools.partial(kernel, npq, nhh, factor),
            out_shape=(
                jax.ShapeDtypeStruct(left_amps.shape, bf16),
                jax.ShapeDtypeStruct((roots, roots), f32),
            ),
            in_specs=[pl.BlockSpec(memory_space=pl.ANY)] * 3,
            out_specs=(
                pl.BlockSpec(memory_space=pl.ANY),
                pl.BlockSpec(memory_space=pltpu.VMEM),
            ),
            scratch_shapes=[
                pltpu.VMEM((npq, rows, depth), bf16),
                pltpu.VMEM((npq, rows, depth), bf16),
                pltpu.VMEM((rows, wide), bf16),
                pltpu.VMEM((SLOTS, depth, wide), f32),
                pltpu.VMEM((SLOTS, half, wide), f32),
                pltpu.VMEM((SLOTS, half, wide), bf16),
                pltpu.VMEM((SLOTS, ny - 1, half, wide), bf16),
                pltpu.VMEM((2, npq, depth, wide), bf16),
                pltpu.VMEM((rows, wide), f32),
                pltpu.VMEM((rows, wide), bf16),
                pltpu.VMEM((roots, wide), f32),
                pltpu.VMEM((nhh + npq, roots, 128), f32),
                dma((2 + roots,)),
                dma((roots,)),
                dma((2, npq, 4)),
                dma((2, npq)),
                dma((SLOTS,)),
                dma((SLOTS,)),
                dma((SLOTS, ny - 1)),
                dma((SLOTS, ny - 1)),
                dma((npq,)),
                dma((npq,)),
                dma((nhh + npq,)),
                dma((nhh + npq,)),
            ],
            compiler_params=pltpu.CompilerParams(
                collective_id=0,
                has_side_effects=True,
                vmem_limit_bytes=67043328,
            ),
        )(amplitudes, integrals, left_amps)

    return jax.shard_map(
        body,
        mesh=mesh,
        in_specs=(P("hh", "pq"), P("hh", "pq"), P(None, "hh", "pq")),
        out_specs=(P(None, "hh", "pq"), P()),
        check_vma=False,
    )
```

time: 575 us -> 125 us (0.22)
  waiting for transfers between devices: 492 us -> 0 us
  Pallas kernels: 0 us -> 120 us
  blocking collectives: 38.4 us -> 0 us
  matrix products: 25.9 us -> 0 us
  between operations: 13.8 us -> 0.65 us
    reduce_scatter x1 -> x0, waiting for transfers between devices: 280 us -> none  [body(): lax.psum_scatter(partial_t, 'pq', scatter_dimension=1, tiled=True)]
    all_gather x3 -> x0, waiting for transfers between devices: 211 us -> none  [the longest x1 127 us: body(): ladder_t = lax.all_gather(ladder_t, 'pq', axis=1, tiled=True)]
    pallas_call x0 -> x1, Pallas kernels: none -> 120 us  [body(): pl.pallas_call(functools.partial(kernel, npq, nhh, factor), out_shape=(ja...]
    psum x1 -> x0, blocking collectives: 38.4 us -> none  [body(): subspace = lax.psum(local_gram, ('pq', 'hh')) * factor]
    dot_general x3 -> x0, matrix products: 25.9 us -> none  [the longest x1 13.7 us: body(): lax.dot_general(ladder_t, lax.all_gather(left_amps, 'hh', axis=1, tiled=T...]
  transfers between devices with their start and end apart: 4 -> 0, of which waited for: 4 -> 0; matrix products, arithmetic and copies ran while one was open for 0% -> 0% of each run, Pallas kernels for 0% -> 0%
where the time goes in v1:
time: 125 us
  Pallas kernels  120 us (96%)
  local copies, waits for them, and re-layouts  3.66 us (3%)
    pallas_call x1, Pallas kernels, body(): pl.pallas_call(functools.partial(kernel, npq, nhh, factor), out_shape=(ja...  120 us
    unnamed x4, local copies, waits for them, and re-layouts  3.66 us

profile of v1, /device:TPU:0, one launch (start us, length us, event | category | flops | bytes accessed | tf_op | source)
XLA Modules:
  0.0 124.5 jit_solution(14193562733538295580)
XLA Ops:
  0.6 120.2 %shard_map.50 = (bf16[8,1024,128]{2,1,0:T(8,128)(2,1)}, f32[8,8]{1,0:T(8,128)}) custom-call(bf16[1024,256]{1,0:T(8,128)(2,1)} %t_ref.1, bf16[1024,256]{1,0:T(8,128)(2,1)} %i_ref.1, bf16[8,1024,128]{2,1,0:T(8,128)(2,1)} %l_ref.1), custom_call_target="tpu_custom_call" | custom-call | tf_op jit(solution)/shard_map/pallas_call | solution.py:298
  120.9 0.0 copy-start
  120.9 3.1 %copy.7 = bf16[8,1024,128]{2,1,0:T(8,128)(2,1)} copy(bf16[8,1024,128]{2,1,0:T(8,128)(2,1)} %get-tuple-element.4) | data formatting | bytes 4194304
  123.9 0.0 copy-done
  123.9 0.6 copy.8
Async XLA Ops:
  120.9 3.1 %copy-start = (f32[8,8]{1,0:T(8,128)S(1)}, f32[8,8]{1,0:T(8,128)}, u32[]{:S(2)}) copy-start(f32[8,8]{1,0:T(8,128)} %get-tuple-element.5) | copy-start | bytes 772

commit v2 on v1

--- a/solution.py
+++ b/solution.py
@@ -81,14 +81,20 @@
             buf, buf, fwd_sem.at[kind, blk, way], blk_sem.at[kind, blk], {"pq": to}
         )
 
-    def ways(zz, xx):
+    balanced = nx == 2 and nz % 2 == 0
+    partner = z + 1 - 2 * (z % 2)
+
+    def ways(kind, zz, xx):
         if xx is None:
+            cross = (zz != partner) if balanced and kind == 1 else (zz >= 0)
             return [
-                (2, x < nx - 1),
-                (3, x > 0),
+                (2, (x < nx - 1) & cross),
+                (3, (x > 0) & cross),
                 (0, (zz <= z) & (z < nz - 1)),
                 (1, (zz >= z) & (z > 0)),
             ]
+        if balanced and kind == 1:
+            return [(0, (zz == z) & (partner > z)), (1, (zz == z) & (partner < z))]
         if nx == 2:
             return []
         return [(2, (xx < x) & (x < nx - 1)), (3, (xx > x) & (x > 0))]
@@ -98,14 +104,14 @@
 
     def forward(kind, zz, xx):
         blk = place(zz, xx)
-        for way, cond in ways(zz, xx):
+        for way, cond in ways(kind, zz, xx):
             @pl.when(cond)
             def _():
                 block_copy(kind, blk, way).start()
 
     def sent(kind, zz, xx):
         blk = place(zz, xx)
-        for way, cond in ways(zz, xx):
+        for way, cond in ways(kind, zz, xx):
             @pl.when(cond)
             def _():
                 block_copy(kind, blk, way).wait_send()
@@ -199,16 +205,20 @@
         if i >= 2:
             arrived(1, zs[i - 1], None)
             forward(1, zs[i - 1], None)
+        if i == 2 and balanced:
+            arrived(1, zs[0], xs[0])
+            forward(1, zs[0], xs[0])
     count = len(order)
     stage2(count - 1)
     stage3(count - 2)
     stage3(count - 1)
 
+    first_cross = min(k for k in range(count) if order[k][1] is not None)
     for k in range(count):
         zz, xx = order[k]
         if k > count - 1 - SLOTS:
             m_copy(k).wait_recv()
-        if xx is not None:
+        if xx is not None and not (balanced and k == first_cross):
             arrived(1, zz, xx)
             forward(1, zz, xx)
         blk = place(zz, xx)

time: 125 us -> 132 us (1.056)
  Pallas kernels: 120 us -> 127 us
    pallas_call x1, Pallas kernels: 120 us -> 127 us  [body(): pl.pallas_call(functools.partial(kernel, npq, nhh, factor), out_shape=(ja...]
where the time goes in v2:
time: 132 us; the launch traced here: 131 us
  Pallas kernels  127 us (96%)
  local copies, waits for them, and re-layouts  3.66 us (3%)
    pallas_call x1, Pallas kernels, body(): pl.pallas_call(functools.partial(kernel, npq, nhh, factor), out_shape=(ja...  127 us
    unnamed x4, local copies, waits for them, and re-layouts  3.66 us

profile of v2, /device:TPU:0, one launch (start us, length us, event | category | flops | bytes accessed | tf_op | source)
XLA Modules:
  0.0 131.5 jit_solution(12369667515066205034)
XLA Ops:
  0.6 127.2 %shard_map.50 = (bf16[8,1024,128]{2,1,0:T(8,128)(2,1)}, f32[8,8]{1,0:T(8,128)}) custom-call(bf16[1024,256]{1,0:T(8,128)(2,1)} %t_ref.1, bf16[1024,256]{1,0:T(8,128)(2,1)} %i_ref.1, bf16[8,1024,128]{2,1,0:T(8,128)(2,1)} %l_ref.1), custom_call_target="tpu_custom_call" | custom-call | tf_op jit(solution)/shard_map/pallas_call | solution.py:308
  127.8 0.0 copy-start
  127.8 3.1 %copy.7 = bf16[8,1024,128]{2,1,0:T(8,128)(2,1)} copy(bf16[8,1024,128]{2,1,0:T(8,128)(2,1)} %get-tuple-element.4) | data formatting | bytes 4194304
  130.9 0.0 copy-done
  130.9 0.6 copy.8
Async XLA Ops:
  127.8 3.1 %copy-start = (f32[8,8]{1,0:T(8,128)S(1)}, f32[8,8]{1,0:T(8,128)}, u32[]{:S(2)}) copy-start(f32[8,8]{1,0:T(8,128)} %get-tuple-element.5) | copy-start | bytes 772

commit v3 on v1

--- a/solution.py
+++ b/solution.py
@@ -191,14 +191,19 @@
             stage3(k - 2)
 
     for i in range(nz + 1):
+        ahead = []
         if i < nz:
             t_event(zs[i], None)
+        if i == nz - 1:
+            ahead = range(1, nz - 2)
+        if i == nz:
+            ahead = range(max(1, nz - 2), nz)
+        for j in ahead:
+            arrived(1, zs[j], None)
+            forward(1, zs[j], None)
         if i >= 1:
             for xx in xs:
                 t_event(zs[i - 1], xx)
-        if i >= 2:
-            arrived(1, zs[i - 1], None)
-            forward(1, zs[i - 1], None)
     count = len(order)
     stage2(count - 1)
     stage3(count - 2)

time: 125 us -> 120 us (0.960)
  Pallas kernels: 120 us -> 116 us
    pallas_call x1, Pallas kernels: 120 us -> 116 us  [body(): pl.pallas_call(functools.partial(kernel, npq, nhh, factor), out_shape=(ja...]
where the time goes in v3:
time: 120 us
  Pallas kernels  116 us (97%)
  local copies, waits for them, and re-layouts  3.66 us (3%)
    pallas_call x1, Pallas kernels, body(): pl.pallas_call(functools.partial(kernel, npq, nhh, factor), out_shape=(ja...  116 us
    unnamed x4, local copies, waits for them, and re-layouts  3.66 us

profile of v3, /device:TPU:0, one launch (start us, length us, event | category | flops | bytes accessed | tf_op | source)
XLA Modules:
  0.0 120.1 jit_solution(5730837459883728089)
XLA Ops:
  0.6 115.8 %shard_map.50 = (bf16[8,1024,128]{2,1,0:T(8,128)(2,1)}, f32[8,8]{1,0:T(8,128)}) custom-call(bf16[1024,256]{1,0:T(8,128)(2,1)} %t_ref.1, bf16[1024,256]{1,0:T(8,128)(2,1)} %i_ref.1, bf16[8,1024,128]{2,1,0:T(8,128)(2,1)} %l_ref.1), custom_call_target="tpu_custom_call" | custom-call | tf_op jit(solution)/shard_map/pallas_call | solution.py:303
  116.4 0.0 copy-start
  116.4 3.1 %copy.7 = bf16[8,1024,128]{2,1,0:T(8,128)(2,1)} copy(bf16[8,1024,128]{2,1,0:T(8,128)(2,1)} %get-tuple-element.4) | data formatting | bytes 4194304
  119.5 0.0 copy-done
  119.5 0.6 copy.8
Async XLA Ops:
  116.4 3.1 %copy-start = (f32[8,8]{1,0:T(8,128)S(1)}, f32[8,8]{1,0:T(8,128)}, u32[]{:S(2)}) copy-start(f32[8,8]{1,0:T(8,128)} %get-tuple-element.5) | copy-start | bytes 772
